TPU v7x, 32 devices: a whole 2x2x4 slice. The times are simulated.
32 devices in a mesh: parts: 2 (over y), section: 2 (over core), tp: 8 (over z, x).
Axes of the slice: x: 2, y: 2, z: 4, core: 2. Of those that a mesh axis runs over, the one named last changes fastest.
Arguments:
- prompt_rows: bfloat16 [128, 8192], P(('parts', 'section', 'tp')), parts along dimension 0, may hold values from -72 to 72
- query_weight: bfloat16 [8192, 8192], P(None, 'tp'), may hold values from -0.0625 to 0.0625
- cache_weight: bfloat16 [8, 8192, 256], P('tp'), may hold values from -1 to 1, as said below
- output_weight: bfloat16 [8192, 8192], P('tp'), may hold values from -0.0625 to 0.0625
- documents: int32 [128], P('parts'), parts along dimension 0, may hold values from 0 to 3, never falling along the last dimension, each value on 1 to 32 neighbouring positions
- page_table: int32 [24], P('parts'), parts along dimension 0, may hold values from 0 to 15, as said below
Outputs:
- branch_output: bfloat16 [128, 8192], P(('parts', 'section', 'tp')), parts along dimension 0
- page_pool: bfloat16 [32, 8, 2048], P(('parts', 'section', 'tp')), parts along dimension 0
There are 2 independent parts, one for each index of `parts`. A program takes and returns all parts, laid end to end along the dimension named above; an argument that names none is the same for every part. Nothing has to cross between parts.
Inputs may be any that keep to these rules, and one draw needn't show every extreme that they name: `cache_weight`: entry t equals entry u whenever t == u. `documents`: ids never fall along the tokens; there are 4 prompts of 1 to 32 tokens, one of exactly 32. `page_table`: entries are distinct pool slots; slot q is owned by the device of index q along section+tp (one slot per device). Entries beyond the number of pages are not used.
All inputs are finite; a program needn't handle non-finite values.
Results may differ from a plain program's by a relative error of at most 0.0085.
The roundings to bfloat16 on the way count: a program that leaves them out, or rounds other values in their place, can miss the bound.
Values may be sent and summed in bfloat16 or wider, within the bound.
No kernel may reach another device: no remote copies, remote signals or barrier semaphores. Data moves between devices by JAX's collectives and lax.ppermute only.
A program may use at most 64 MiB of HBM per device.

v0:
```python
import jax
import jax.numpy as jnp
from jax import lax
from jax.sharding import PartitionSpec as P

KV_HEADS = 8
HEAD = 128
PAGE = 8
FEW = 8
rope_base = 500000.0


def from_partner(value, axis, mask):
    pairs = [(source, source ^ mask) for source in range(lax.axis_size(axis))]
    return lax.ppermute(value, axis, pairs)


def few_devices(count):
    return 4 <= count <= FEW and count & count - 1 == 0


def gather_rows(rows):
    count = lax.axis_size("tp")
    if not few_devices(count):
        return lax.all_gather(rows, "tp", axis=0, tiled=True)
    column = lax.axis_index("tp")
    blocks = {0: rows}
    for mask in range(2, count, 2):
        blocks[mask] = from_partner(rows, "tp", mask)
    for mask in range(0, count, 2):
        blocks[mask + 1] = from_partner(blocks[mask], "tp", 1)
    stacked = jnp.stack([blocks[mask] for mask in range(count)], axis=0)
    pieces = []
    for place in range(count):
        piece = lax.dynamic_index_in_dim(stacked, place ^ column, 0, keepdims=False)
        pieces.append(piece)
    return jnp.concatenate(pieces, axis=0)


def scatter_sum(partial, rows_dev):
    count = lax.axis_size("tp")
    if not few_devices(count):
        return lax.psum_scatter(partial, "tp", scatter_dimension=0, tiled=True)
    column = lax.axis_index("tp")
    blocks = partial.reshape(count, rows_dev, partial.shape[1])
    total = lax.dynamic_index_in_dim(blocks, column, 0, keepdims=False)
    narrow = blocks.astype(jnp.bfloat16)
    for mask in range(count - 1, 0, -1):
        sent = lax.dynamic_index_in_dim(narrow, column ^ mask, 0, keepdims=False)
        total = total + from_partner(sent, "tp", mask).astype(jnp.float32)
    return total


def document_layout(documents):
    count = documents.shape[0]
    places = jnp.arange(count, dtype=jnp.int32)
    firsts = jnp.sum((documents[None, :] < documents[:, None]).astype(jnp.int32), axis=1)
    offsets = places - firsts
    starts = (offsets % PAGE == 0)[None, :] & (places[None, :] <= places[:, None])
    pages = jnp.sum(starts.astype(jnp.int32), axis=1) - 1
    return (offsets, pages)


def rope_tables(offsets, width):
    half_width = width // 2
    freqs = rope_base ** (-(jnp.arange(half_width, dtype=jnp.float32) * 2.0 / width))
    angles = offsets.astype(jnp.float32)[:, None] * freqs[None, :]
    return (jnp.cos(angles), jnp.sin(angles))


def rotate(values, cosines, sines):
    half_width = values.shape[-1] // 2
    first = values[..., :half_width]
    second = values[..., half_width:]
    return jnp.concatenate(
        [first * cosines - second * sines, second * cosines + first * sines], axis=-1
    )


def finish_cache(keyvals, cosines, sines):
    rotated = rotate(keyvals[:, :HEAD], cosines, sines)
    return jnp.concatenate([rotated, keyvals[:, HEAD:]], axis=1).astype(jnp.bfloat16)


def body(prompt_rows, query_weight, cache_weight, output_weight, documents, page_table):
    tp_count = lax.axis_size("tp")
    owners = lax.axis_size(("section", "tp"))
    section = lax.axis_index("section")
    column = lax.axis_index("tp")
    rows_dev = prompt_rows.shape[0]
    half_rows = rows_dev * tp_count
    total_rows = 2 * half_rows
    query_width = query_weight.shape[1]
    query_heads = query_width // HEAD
    replicas = tp_count // KV_HEADS
    slice_width = HEAD // replicas
    head_weight = cache_weight[0]
    offsets, pages = document_layout(documents)
    cosines, sines = rope_tables(offsets, HEAD)
    own_start = section * half_rows
    own_cos = lax.dynamic_slice_in_dim(cosines, own_start, half_rows, 0)
    own_sin = lax.dynamic_slice_in_dim(sines, own_start, half_rows, 0)
    piece = gather_rows(prompt_rows)
    cache_rows = jnp.dot(piece, head_weight, preferred_element_type=jnp.float32)
    query_part = jnp.dot(piece, query_weight, preferred_element_type=jnp.float32)
    cache_half = finish_cache(cache_rows, own_cos, own_sin)
    other = from_partner(cache_half, "section", 1)
    lower = jnp.where(section == 0, cache_half, other)
    upper = jnp.where(section == 0, other, cache_half)
    cache_all = jnp.concatenate([lower, upper], axis=0)
    queries = query_part.reshape(half_rows, query_heads, HEAD)
    queries = rotate(queries, own_cos[:, None, :], own_sin[:, None, :]).astype(jnp.bfloat16)
    keys = cache_all[:, :HEAD]
    values = cache_all[:, HEAD:]
    places = jnp.arange(total_rows, dtype=jnp.int32)
    query_places = own_start + jnp.arange(half_rows, dtype=jnp.int32)
    query_docs = lax.dynamic_slice_in_dim(documents, own_start, half_rows, 0)
    allowed = (query_docs[:, None] == documents[None, :]) & (
        places[None, :] <= query_places[:, None]
    )
    scale = 1.0 / HEAD**0.5
    scores = jnp.einsum("qhd,kd->hqk", queries, keys, preferred_element_type=jnp.float32) * scale
    scores = jnp.where(allowed[None, :, :], scores, -jnp.inf)
    weights = jax.nn.softmax(scores, axis=-1).astype(jnp.bfloat16)
    mixed = jnp.einsum("hqk,kd->qhd", weights, values, preferred_element_type=jnp.float32)
    attention = mixed.astype(jnp.bfloat16).reshape(half_rows, query_heads * HEAD)
    column_start = section * HEAD + column % replicas * slice_width
    share = lax.dynamic_slice_in_dim(cache_all, column_start, slice_width, 1)
    capacity = rows_dev // 4 * PAGE
    slots = jnp.arange(page_table.shape[0], dtype=jnp.int32)
    hit = pages[:, None] == slots[None, :]
    table_at = jnp.sum(jnp.where(hit, page_table[None, :], 0), axis=1)
    row_of = table_at * PAGE + offsets % PAGE
    pool_rows = jnp.arange(owners * capacity, dtype=jnp.int32)
    placed = (pool_rows[:, None] == row_of[None, :]).astype(jnp.bfloat16)
    outgoing = jnp.dot(placed, share, preferred_element_type=jnp.float32).astype(jnp.bfloat16)
    outgoing = outgoing.reshape(owners, capacity, slice_width)
    arrived = lax.all_to_all(outgoing, ("section", "tp"), split_axis=0, concat_axis=2, tiled=True)
    partial = jnp.dot(attention, output_weight, preferred_element_type=jnp.float32)
    branch_output = scatter_sum(partial, rows_dev).astype(jnp.bfloat16)
    return (branch_output, arrived)


def solution(mesh):
    return jax.shard_map(
        body,
        mesh=mesh,
        in_specs=(
            P(("parts", "section", "tp"), None),
            P(None, "tp"),
            P("tp", None, None),
            P("tp", None),
            P("parts"),
            P("parts"),
        ),
        out_specs=(P(("parts", "section", "tp"), None), P(("parts", "section", "tp"), None, None)),
        check_vma=False,
    )
```

profile of v0, /device:TPU:0, one launch (start us, length us, event | category | flops | bytes accessed | tf_op | source)
XLA Modules:
  0.0 67.6 jit_solution(11010513600274081855)
XLA Ops:
  0.6 3.1 %collective-permute-start.1 = (bf16[4,8192]{1,0:T(4,128)(2,1)}, bf16[4,8192]{1,0:T(4,128)(2,1)S(1)}, u32[]{:S(2)}, u32[]{:S(2)}) collective-permute-start(bf16[4,8192]{1,0:T(4,128)(2,1)} %param.6), channel_id=1, source_target_pairs={{0,2},{1,3},{2,0},{3,1},{4,6},{5,7},{6,4},{7,5},{8,10},{9,11},{10,... | collective-permute-start | bytes 196616 | tf_op jit(solution)/shard_map/ppermute | solution.py:15
  3.7 1.5 %collective-permute-start = (bf16[4,8192]{1,0:T(4,128)(2,1)}, bf16[4,8192]{1,0:T(4,128)(2,1)S(1)}, u32[]{:S(2)}, u32[]{:S(2)}) collective-permute-start(bf16[4,8192]{1,0:T(4,128)(2,1)} %param.6), channel_id=1, source_target_pairs={{0,1},{1,0},{2,3},{3,2},{4,5},{5,4},{6,7},{7,6},{8,9},{9,8},{10,11... | collective-permute-start | bytes 196616 | tf_op jit(solution)/shard_map/ppermute | solution.py:15
  5.2 2.5 %collective-permute-start.5 = (bf16[4,8192]{1,0:T(4,128)(2,1)}, bf16[4,8192]{1,0:T(4,128)(2,1)S(1)}, u32[]{:S(2)}, u32[]{:S(2)}) collective-permute-start(bf16[4,8192]{1,0:T(4,128)(2,1)} %param.6), channel_id=1, source_target_pairs={{0,6},{1,7},{2,4},{3,5},{4,2},{5,3},{6,0},{7,1},{8,14},{9,15},{10,... | collective-permute-start | bytes 196616 | tf_op jit(solution)/shard_map/ppermute | solution.py:15
  7.7 0.1 collective-permute-start.3
  7.8 0.9 %convert_reduce_fusion.1 = s32[64]{0:T(128)S(1)} fusion(s32[64]{0:T(128)} %param.10), kind=kLoop, calls=%fused_computation.63 | loop fusion | flops 12224 | bytes 512 | tf_op jit(solution)/shard_map/reduce_sum | solution.py:57
  8.8 0.9 %bitcast_dynamic-update-slice_fusion.7 = bf16[8,4,8192]{2,1,0:T(4,128)(2,1)S(1)} fusion(bf16[4,8192]{1,0:T(4,128)(2,1)} %param.6), kind=kLoop, calls=%fused_computation.43 | loop fusion | bytes 131072
  9.7 0.7 %dynamic_slice.72 = s32[32]{0:T(128)S(1)} dynamic-slice(s32[64]{0:T(128)} %param.10, s32[]{:T(128)S(6)} %select_n.91), dynamic_slice_sizes={32} | dynamic-slice | bytes 260 | tf_op jit(solution)/shard_map/dynamic_slice | solution.py:117
  10.4 0.1 convert_reduce_fusion
  10.5 0.7 %select_reduce_fusion = s32[64]{0:T(128)S(1)} fusion(s32[12]{0:T(128)} %param.11, s32[64]{0:T(128)S(1)} %broadcast_add_fusion), kind=kLoop, calls=%fused_computation.81 | loop fusion | flops 2240 | bytes 560 | tf_op jit(solution)/shard_map/reduce_sum | solution.py:132
  11.3 0.7 %fusion.32 = pred[32,64]{1,0:T(8,128)(4,1)S(1)} fusion(s32[32]{0:T(128)S(1)} %iota_add_fusion, s32[64]{0:T(128)} %param.10, s32[32]{0:T(128)S(1)} %dynamic_slice.72), kind=kLoop, calls=%fused_computation.76 | loop fusion | flops 6144 | bytes 2560 | tf_op jit(solution)/shard_map/and | solution.py:118
  12.0 0.1 broadcast_multiply_fusion
  12.1 0.0 collective-permute-done.1
  12.1 0.6 collective-permute-start.2
  12.7 0.0 collective-permute-done.5
  12.7 1.5 %collective-permute-start.6 = (bf16[4,8192]{1,0:T(4,128)(2,1)S(1)}, bf16[4,8192]{1,0:T(4,128)(2,1)S(1)}, u32[]{:S(2)}, u32[]{:S(2)}) collective-permute-start(bf16[4,8192]{1,0:T(4,128)(2,1)S(1)} %collective-permute-done.5), channel_id=1, source_target_pairs={{0,1},{1,0},{2,3},{3,2},{4,5},{5,4},{6,7},{7,6},{8,9},{9,8},{10,11... | collective-permute-start | bytes 196616 | tf_op jit(solution)/shard_map/ppermute | solution.py:15
  14.2 0.0 collective-permute-done.3
  14.2 0.6 collective-permute-start.4
  14.8 0.0 collective-permute-done
  14.9 1.7 %collective-permute-done.2 = bf16[4,8192]{1,0:T(4,128)(2,1)S(1)} collective-permute-done((bf16[4,8192]{1,0:T(4,128)(2,1)S(1)}, bf16[4,8192]{1,0:T(4,128)(2,1)S(1)}, u32[]{:S(2)}, u32[]{:S(2)}) %collective-permute-start.2) | collective-permute-done | bytes 65568 | tf_op jit(solution)/shard_map/ppermute | solution.py:15
  16.7 1.9 %collective-permute-done.4 = bf16[4,8192]{1,0:T(4,128)(2,1)S(1)} collective-permute-done((bf16[4,8192]{1,0:T(4,128)(2,1)S(1)}, bf16[4,8192]{1,0:T(4,128)(2,1)S(1)}, u32[]{:S(2)}, u32[]{:S(2)}) %collective-permute-start.4) | collective-permute-done | bytes 65568 | tf_op jit(solution)/shard_map/ppermute | solution.py:15
  18.6 0.0 collective-permute-done.6
  18.7 0.2 dynamic-slice_bitcast_fusion
  18.9 0.3 concatenate.14
  19.3 3.0 %fusion.3 = f32[32,256]{1,0:T(8,128)S(1)} fusion(bf16[32,8192]{1,0:T(8,128)(2,1)S(1)} %concatenate.14, bf16[1,8192,256]{2,1,0:T(8,128)(2,1)} %param.8), kind=kOutput, calls=%fused_computation.3 | convolution fusion | flops 134217728 | bytes 4751360 | tf_op jit(solution)/shard_map/dot_general | solution.py:104
  22.3 8.8 %convolution_bitcast_fusion = f32[4,8,8,128]{3,1,2,0:T(8,128)S(1)} fusion(bf16[32,8192]{1,0:T(8,128)(2,1)S(1)} %concatenate.14, bf16[8192,1024]{1,0:T(8,128)(2,1)} %param.7), kind=kOutput, calls=%fused_computation.7 | convolution fusion | flops 536870912 | bytes 17432576 | tf_op jit(solution)/shard_map/dot_general | solution.py:105
  31.1 0.1 subtract_convert_fusion.1
  31.2 0.1 add_convert_fusion.1
  31.2 0.1 pad_maximum_fusion
  31.3 0.0 collective-permute-start.7
  31.3 0.1 fusion.66
  31.4 0.1 subtract_convert_fusion
  31.5 1.0 %collective-permute-done.7 = bf16[32,256]{1,0:T(8,128)(2,1)S(1)} collective-permute-done((bf16[32,256]{1,0:T(8,128)(2,1)S(1)}, bf16[32,256]{1,0:T(8,128)(2,1)S(1)}, u32[]{:S(2)}, u32[]{:S(2)}) %collective-permute-start.7) | collective-permute-done | bytes 16416 | tf_op jit(solution)/shard_map/ppermute | solution.py:15
  32.5 0.1 broadcast_select_fusion
  32.6 0.4 fusion.67
  33.0 0.6 fusion.9
  33.6 8.6 %fusion.72 = (bf16[8,4,8192]{2,0,1:T(8,128)(2,1)S(1)}, f32[8,4,8192]{2,0,1:T(8,128)S(1)}) fusion(bf16[1024,8192]{1,0:T(8,128)(2,1)} %param.9, bf16[8,4,1024]{2,1,0:T(4,128)(2,1)S(1)} %dot_general.24), kind=kOutput, calls=%fused_computation.114 | convolution fusion | flops 537133056 | bytes 18415616 | tf_op jit(solution)/shard_map/dot_general | solution.py:139
  42.3 1.0 %constant_dynamic-slice_fusion.6 = (bf16[1,4,8192]{2,0,1:T(2,128)(2,1)S(1)}, bf16[1,4,8192]{2,0,1:T(2,128)(2,1)S(1)}, bf16[1,4,8192]{2,0,1:T(2,128)(2,1)S(1)}, b...) fusion(bf16[8,4,8192]{2,0,1:T(8,128)(2,1)S(1)} %get-tuple-eleme, ...), kind=kLoop, calls=%fused_computation.89 | loop fusion | bytes 917532 | tf_op jit(solution)/shard_map/jit(dynamic_index_in_dim)/dynamic_slice | solution.py:49
  43.3 0.1 copy.51
  43.4 0.1 copy.52
  43.5 2.9 %collective-permute-start.9 = (bf16[4,8192]{1,0:T(4,128)(2,1)S(1)}, bf16[4,8192]{1,0:T(4,128)(2,1)S(1)}, u32[]{:S(2)}, u32[]{:S(2)}) collective-permute-start(bf16[4,8192]{1,0:T(4,128)(2,1)S(1)} %bitcast.129), channel_id=1, source_target_pairs={{0,6},{1,7},{2,4},{3,5},{4,2},{5,3},{6,0},{7,1},{8,14},{9,15},{10,... | collective-permute-start | bytes 196616 | tf_op jit(solution)/shard_map/ppermute | solution.py:15
  46.4 0.5 collective-permute-start.10
  46.9 0.7 %fusion.10 = bf16[16,8,128]{2,1,0:T(8,128)(2,1)} fusion(s32[64]{0:T(128)S(1)} %multiply_add_fusion, s32[]{:T(128)S(6)} %select_n.97, bf16[32,256]{1,0:T(8,128)(2,1)S(1)} %get-tuple-element.27, bf16[32,256]{1,0:T(8,128)(2,1)S(1)} %get-tuple-element.26), kind=kOutput, calls=%fused_computation.14 | convolution fusion | flops 2154496 | bytes 65796 | tf_op jit(solution)/shard_map/dot_general | solution.py:136
  47.6 4.7 %all-to-all-start = ((bf16[16,8,128]{2,1,0:T(8,128)(2,1)}), bf16[16,8,128]{2,1,0:T(8,128)(2,1)S(1)}, u32[]{:S(2)}, u32[]{:S(2)}) async-start(bf16[16,8,128]{2,1,0:T(8,128)(2,1)} %fusion.10), calls=%async_computation | async-start | bytes 65536 | tf_op jit(solution)/shard_map/all_to_all | solution.py:138
  52.4 0.1 copy.53
  52.5 0.1 copy.47
  52.6 0.1 copy.48
  52.7 0.1 copy.49
  52.8 0.1 copy.50
  52.9 2.9 %collective-permute-start.11 = (bf16[4,8192]{1,0:T(4,128)(2,1)S(1)}, bf16[4,8192]{1,0:T(4,128)(2,1)S(1)}, u32[]{:S(2)}, u32[]{:S(2)}) collective-permute-start(bf16[4,8192]{1,0:T(4,128)(2,1)S(1)} %bitcast.130), channel_id=1, source_target_pairs={{0,4},{1,5},{2,6},{3,7},{4,0},{5,1},{6,2},{7,3},{8,12},{9,13},{10,... | collective-permute-start | bytes 196616 | tf_op jit(solution)/shard_map/ppermute | solution.py:15
  55.7 2.4 %collective-permute-start.12 = (bf16[4,8192]{1,0:T(4,128)(2,1)S(1)}, bf16[4,8192]{1,0:T(4,128)(2,1)S(1)}, u32[]{:S(2)}, u32[]{:S(2)}) collective-permute-start(bf16[4,8192]{1,0:T(4,128)(2,1)S(1)} %bitcast.128), channel_id=1, source_target_pairs={{0,3},{1,2},{2,1},{3,0},{4,7},{5,6},{6,5},{7,4},{8,11},{9,10},{10,... | collective-permute-start | bytes 196616 | tf_op jit(solution)/shard_map/ppermute | solution.py:15
  58.1 0.6 collective-permute-start.13
  58.7 0.0 collective-permute-done.9
  58.7 0.6 collective-permute-start.14
  59.2 0.0 collective-permute-done.10
  59.2 2.4 %collective-permute-start.8 = (bf16[4,8192]{1,0:T(4,128)(2,1)S(1)}, bf16[4,8192]{1,0:T(4,128)(2,1)S(1)}, u32[]{:S(2)}, u32[]{:S(2)}) collective-permute-start(bf16[4,8192]{1,0:T(4,128)(2,1)S(1)} %bitcast.124), channel_id=1, source_target_pairs={{0,7},{1,6},{2,5},{3,4},{4,3},{5,2},{6,1},{7,0},{8,15},{9,14},{10,... | collective-permute-start | bytes 196616 | tf_op jit(solution)/shard_map/ppermute | solution.py:15
  61.6 0.1 constant_dynamic-slice_fusion.7
  61.7 0.0 all-to-all-done
  61.7 0.0 collective-permute-done.11
  61.7 0.4 collective-permute-done.12
  62.1 0.4 collective-permute-done.13
  62.5 0.4 collective-permute-done.14
  62.9 3.3 %collective-permute-done.8 = bf16[4,8192]{1,0:T(4,128)(2,1)S(1)} collective-permute-done((bf16[4,8192]{1,0:T(4,128)(2,1)S(1)}, bf16[4,8192]{1,0:T(4,128)(2,1)S(1)}, u32[]{:S(2)}, u32[]{:S(2)}) %collective-permute-start.8) | collective-permute-done | bytes 65568 | tf_op jit(solution)/shard_map/ppermute | solution.py:15
  66.2 0.8 %fusion.17 = bf16[4,8192]{1,0:T(4,128)(2,1)} fusion(bf16[4,8192]{1,0:T(4,128)(2,1)S(1)} %collective-permute-done.14, bf16[4,8192]{1,0:T(4,128)(2,1)S(1)} %collective-permute-done.13, bf16[4,8192]{1,0:T(4,128)(2,1)S(1)} %collective-permute-done.12, bf16[4,8192]{1,0:T(4,128)(2,1)S(1)} %collective-permute-done.11, ...), kind=kLoop, calls=%fused_computation.25 | loop fusion | flops 491520 | bytes 655360 | tf_op jit(solution)/shard_map/convert_element_type | solution.py:140
  67.0 0.6 copy.62
  (17 shorter events, 0.4 us)
Async XLA Ops:
  0.6 11.5 %collective-permute-start.1 = (bf16[4,8192]{1,0:T(4,128)(2,1)}, bf16[4,8192]{1,0:T(4,128)(2,1)S(1)}, u32[]{:S(2)}, u32[]{:S(2)}) collective-permute-start(bf16[4,8192]{1,0:T(4,128)(2,1)} %param.6), channel_id=1, source_target_pairs={{0,2},{1,3},{2,0},{3,1},{4,6},{5,7},{6,4},{7,5},{8,10},{9,11},{10,... | collective-permute-start | bytes 196616 | tf_op jit(solution)/shard_map/ppermute | solution.py:15
  3.7 11.1 %collective-permute-start = (bf16[4,8192]{1,0:T(4,128)(2,1)}, bf16[4,8192]{1,0:T(4,128)(2,1)S(1)}, u32[]{:S(2)}, u32[]{:S(2)}) collective-permute-start(bf16[4,8192]{1,0:T(4,128)(2,1)} %param.6), channel_id=1, source_target_pairs={{0,1},{1,0},{2,3},{3,2},{4,5},{5,4},{6,7},{7,6},{8,9},{9,8},{10,11... | collective-permute-start | bytes 196616 | tf_op jit(solution)/shard_map/ppermute | solution.py:15
  5.2 7.5 %collective-permute-start.5 = (bf16[4,8192]{1,0:T(4,128)(2,1)}, bf16[4,8192]{1,0:T(4,128)(2,1)S(1)}, u32[]{:S(2)}, u32[]{:S(2)}) collective-permute-start(bf16[4,8192]{1,0:T(4,128)(2,1)} %param.6), channel_id=1, source_target_pairs={{0,6},{1,7},{2,4},{3,5},{4,2},{5,3},{6,0},{7,1},{8,14},{9,15},{10,... | collective-permute-start | bytes 196616 | tf_op jit(solution)/shard_map/ppermute | solution.py:15
  7.7 6.5 %collective-permute-start.3 = (bf16[4,8192]{1,0:T(4,128)(2,1)}, bf16[4,8192]{1,0:T(4,128)(2,1)S(1)}, u32[]{:S(2)}, u32[]{:S(2)}) collective-permute-start(bf16[4,8192]{1,0:T(4,128)(2,1)} %param.6), channel_id=1, source_target_pairs={{0,4},{1,5},{2,6},{3,7},{4,0},{5,1},{6,2},{7,3},{8,12},{9,13},{10,... | collective-permute-start | bytes 196616 | tf_op jit(solution)/shard_map/ppermute | solution.py:15
  12.1 4.5 %collective-permute-start.2 = (bf16[4,8192]{1,0:T(4,128)(2,1)S(1)}, bf16[4,8192]{1,0:T(4,128)(2,1)S(1)}, u32[]{:S(2)}, u32[]{:S(2)}) collective-permute-start(bf16[4,8192]{1,0:T(4,128)(2,1)S(1)} %collective-permute-done.1), channel_id=1, source_target_pairs={{0,1},{1,0},{2,3},{3,2},{4,5},{5,4},{6,7},{7,6},{8,9},{9,8},{10,11... | collective-permute-start | bytes 196616 | tf_op jit(solution)/shard_map/ppermute | solution.py:15
  12.7 5.9 %collective-permute-start.6 = (bf16[4,8192]{1,0:T(4,128)(2,1)S(1)}, bf16[4,8192]{1,0:T(4,128)(2,1)S(1)}, u32[]{:S(2)}, u32[]{:S(2)}) collective-permute-start(bf16[4,8192]{1,0:T(4,128)(2,1)S(1)} %collective-permute-done.5), channel_id=1, source_target_pairs={{0,1},{1,0},{2,3},{3,2},{4,5},{5,4},{6,7},{7,6},{8,9},{9,8},{10,11... | collective-permute-start | bytes 196616 | tf_op jit(solution)/shard_map/ppermute | solution.py:15
  14.2 4.3 %collective-permute-start.4 = (bf16[4,8192]{1,0:T(4,128)(2,1)S(1)}, bf16[4,8192]{1,0:T(4,128)(2,1)S(1)}, u32[]{:S(2)}, u32[]{:S(2)}) collective-permute-start(bf16[4,8192]{1,0:T(4,128)(2,1)S(1)} %collective-permute-done.3), channel_id=1, source_target_pairs={{0,1},{1,0},{2,3},{3,2},{4,5},{5,4},{6,7},{7,6},{8,9},{9,8},{10,11... | collective-permute-start | bytes 196616 | tf_op jit(solution)/shard_map/ppermute | solution.py:15
  31.3 1.2 %collective-permute-start.7 = (bf16[32,256]{1,0:T(8,128)(2,1)S(1)}, bf16[32,256]{1,0:T(8,128)(2,1)S(1)}, u32[]{:S(2)}, u32[]{:S(2)}) collective-permute-start(bf16[32,256]{1,0:T(8,128)(2,1)S(1)} %pad_maximum_fusion), channel_id=1, source_target_pairs={{0,8},{8,0},{1,9},{9,1},{2,10},{10,2},{3,11},{11,3},{4,12},{12,4},... | collective-permute-start | bytes 49160 | tf_op jit(solution)/shard_map/ppermute | solution.py:15
  43.5 15.2 %collective-permute-start.9 = (bf16[4,8192]{1,0:T(4,128)(2,1)S(1)}, bf16[4,8192]{1,0:T(4,128)(2,1)S(1)}, u32[]{:S(2)}, u32[]{:S(2)}) collective-permute-start(bf16[4,8192]{1,0:T(4,128)(2,1)S(1)} %bitcast.129), channel_id=1, source_target_pairs={{0,6},{1,7},{2,4},{3,5},{4,2},{5,3},{6,0},{7,1},{8,14},{9,15},{10,... | collective-permute-start | bytes 196616 | tf_op jit(solution)/shard_map/ppermute | solution.py:15
  46.4 12.8 %collective-permute-start.10 = (bf16[4,8192]{1,0:T(4,128)(2,1)S(1)}, bf16[4,8192]{1,0:T(4,128)(2,1)S(1)}, u32[]{:S(2)}, u32[]{:S(2)}) collective-permute-start(bf16[4,8192]{1,0:T(4,128)(2,1)S(1)} %bitcast.126), channel_id=1, source_target_pairs={{0,5},{1,4},{2,7},{3,6},{4,1},{5,0},{6,3},{7,2},{8,13},{9,12},{10,... | collective-permute-start | bytes 196616 | tf_op jit(solution)/shard_map/ppermute | solution.py:15
  47.6 14.1 %all-to-all-start = ((bf16[16,8,128]{2,1,0:T(8,128)(2,1)}), bf16[16,8,128]{2,1,0:T(8,128)(2,1)S(1)}, u32[]{:S(2)}, u32[]{:S(2)}) async-start(bf16[16,8,128]{2,1,0:T(8,128)(2,1)} %fusion.10), calls=%async_computation | async-start | bytes 65536 | tf_op jit(solution)/shard_map/all_to_all | solution.py:138
  52.9 8.9 %collective-permute-start.11 = (bf16[4,8192]{1,0:T(4,128)(2,1)S(1)}, bf16[4,8192]{1,0:T(4,128)(2,1)S(1)}, u32[]{:S(2)}, u32[]{:S(2)}) collective-permute-start(bf16[4,8192]{1,0:T(4,128)(2,1)S(1)} %bitcast.130), channel_id=1, source_target_pairs={{0,4},{1,5},{2,6},{3,7},{4,0},{5,1},{6,2},{7,3},{8,12},{9,13},{10,... | collective-permute-start | bytes 196616 | tf_op jit(solution)/shard_map/ppermute | solution.py:15
  55.7 6.4 %collective-permute-start.12 = (bf16[4,8192]{1,0:T(4,128)(2,1)S(1)}, bf16[4,8192]{1,0:T(4,128)(2,1)S(1)}, u32[]{:S(2)}, u32[]{:S(2)}) collective-permute-start(bf16[4,8192]{1,0:T(4,128)(2,1)S(1)} %bitcast.128), channel_id=1, source_target_pairs={{0,3},{1,2},{2,1},{3,0},{4,7},{5,6},{6,5},{7,4},{8,11},{9,10},{10,... | collective-permute-start | bytes 196616 | tf_op jit(solution)/shard_map/ppermute | solution.py:15
  58.1 4.4 %collective-permute-start.13 = (bf16[4,8192]{1,0:T(4,128)(2,1)S(1)}, bf16[4,8192]{1,0:T(4,128)(2,1)S(1)}, u32[]{:S(2)}, u32[]{:S(2)}) collective-permute-start(bf16[4,8192]{1,0:T(4,128)(2,1)S(1)} %bitcast.127), channel_id=1, source_target_pairs={{0,2},{1,3},{2,0},{3,1},{4,6},{5,7},{6,4},{7,5},{8,10},{9,11},{10,... | collective-permute-start | bytes 196616 | tf_op jit(solution)/shard_map/ppermute | solution.py:15
  58.7 4.3 %collective-permute-start.14 = (bf16[4,8192]{1,0:T(4,128)(2,1)S(1)}, bf16[4,8192]{1,0:T(4,128)(2,1)S(1)}, u32[]{:S(2)}, u32[]{:S(2)}) collective-permute-start(bf16[4,8192]{1,0:T(4,128)(2,1)S(1)} %bitcast.125), channel_id=1, source_target_pairs={{0,1},{1,0},{2,3},{3,2},{4,5},{5,4},{6,7},{7,6},{8,9},{9,8},{10,11... | collective-permute-start | bytes 196616 | tf_op jit(solution)/shard_map/ppermute | solution.py:15
  59.2 7.0 %collective-permute-start.8 = (bf16[4,8192]{1,0:T(4,128)(2,1)S(1)}, bf16[4,8192]{1,0:T(4,128)(2,1)S(1)}, u32[]{:S(2)}, u32[]{:S(2)}) collective-permute-start(bf16[4,8192]{1,0:T(4,128)(2,1)S(1)} %bitcast.124), channel_id=1, source_target_pairs={{0,7},{1,6},{2,5},{3,4},{4,3},{5,2},{6,1},{7,0},{8,15},{9,14},{10,... | collective-permute-start | bytes 196616 | tf_op jit(solution)/shard_map/ppermute | solution.py:15
where the time goes:
time: 68 us; the launch traced here: 67.6 us
  starting transfers between devices  26.7 us (39%)
  matrix products  22.1 us (32%)
  waiting for transfers between devices  9.11 us (13%)
  local copies, waits for them, and re-layouts  4.95 us (7%)
  other arithmetic  3.81 us (6%)
  between operations  0.92 us (1%)
    ppermute x15, starting transfers between devices, from_partner(): return lax.ppermute(value, axis, pairs)  22 us
    ppermute x15, waiting for transfers between devices, from_partner(): return lax.ppermute(value, axis, pairs)  9.11 us
    dot_general x1, matrix products, body(): jnp.dot(piece, query_weight, preferred_element_type=jnp.float32)  8.76 us
    dot_general x1, matrix products, body(): jnp.dot(attention, output_weight, preferred_element_type=jnp.float32)  8.63 us
    all_to_all x1, starting transfers between devices, body(): lax.all_to_all(outgoing, ('section', 'tp'), split_axis=0, concat_axis=2,...  4.73 us
    dot_general x1, matrix products, body(): cache_rows = jnp.dot(piece, head_weight, preferred_element_type=jnp.float32)  3.01 us
    unnamed x16, local copies, waits for them, and re-layouts  2.34 us
  transfers between devices with their start and end apart: 16, of which 7 were waited for; matrix products, arithmetic and copies ran while one was open for 9% of the time, Pallas kernels for 0%

commit v1 on v0

--- a/solution.py
+++ b/solution.py
@@ -135,7 +135,15 @@
     placed = (pool_rows[:, None] == row_of[None, :]).astype(jnp.bfloat16)
     outgoing = jnp.dot(placed, share, preferred_element_type=jnp.float32).astype(jnp.bfloat16)
     outgoing = outgoing.reshape(owners, capacity, slice_width)
-    arrived = lax.all_to_all(outgoing, ("section", "tp"), split_axis=0, concat_axis=2, tiled=True)
+    arrived = jnp.concatenate(
+        lax.all_to_all(
+            jnp.stack(jnp.split(outgoing, lax.axis_size(("section", "tp")), axis=0)),
+            ("section", "tp"),
+            0,
+            0,
+        ),
+        axis=2,
+    )
     partial = jnp.dot(attention, output_weight, preferred_element_type=jnp.float32)
     branch_output = scatter_sum(partial, rows_dev).astype(jnp.bfloat16)
     return (branch_output, arrived)

time: 68 us -> 76.7 us (1.13)
  local copies, waits for them, and re-layouts: 4.95 us -> 14.2 us
    unnamed x16 -> x31, local copies, waits for them, and re-layouts: 2.34 us -> 11 us
  transfers between devices with their start and end apart: 16 -> 16, of which waited for: 7 -> 7; matrix products, arithmetic and copies ran while one was open for 9% -> 7% of each run, Pallas kernels for 0% -> 0%
where the time goes in v1:
time: 76.7 us; the launch traced here: 76.3 us
  starting transfers between devices  26.7 us (35%)
  matrix products  21.5 us (28%)
  local copies, waits for them, and re-layouts  14.2 us (19%)
  waiting for transfers between devices  9.11 us (12%)
  other arithmetic  3.81 us (5%)
  between operations  0.92 us (1%)
    ppermute x15, starting transfers between devices, from_partner(): return lax.ppermute(value, axis, pairs)  22 us
    unnamed x31, local copies, waits for them, and re-layouts  11 us
    ppermute x15, waiting for transfers between devices, from_partner(): return lax.ppermute(value, axis, pairs)  9.11 us
    dot_general x1, matrix products, body(): jnp.dot(piece, query_weight, preferred_element_type=jnp.float32)  8.76 us
    dot_general x1, matrix products, body(): jnp.dot(attention, output_weight, preferred_element_type=jnp.float32)  8.62 us
    all_to_all x1, starting transfers between devices, body(): lax.all_to_all(jnp.stack(jnp.split(outgoing, lax.axis_size(('section', 't...  4.73 us
    dot_general x1, matrix products, body(): cache_rows = jnp.dot(piece, head_weight, preferred_element_type=jnp.float32)  3.01 us
  transfers between devices with their start and end apart: 16, of which 7 were waited for; matrix products, arithmetic and copies ran while one was open for 7% of the time, Pallas kernels for 0%

profile of v1, /device:TPU:0, one launch (start us, length us, event | category | flops | bytes accessed | tf_op | source)
XLA Modules:
  0.0 76.3 jit_solution(11264101624380478542)
XLA Ops:
  0.6 3.1 %collective-permute-start.1 = (bf16[4,8192]{1,0:T(4,128)(2,1)}, bf16[4,8192]{1,0:T(4,128)(2,1)S(1)}, u32[]{:S(2)}, u32[]{:S(2)}) collective-permute-start(bf16[4,8192]{1,0:T(4,128)(2,1)} %param.6), channel_id=1, source_target_pairs={{0,2},{1,3},{2,0},{3,1},{4,6},{5,7},{6,4},{7,5},{8,10},{9,11},{10,... | collective-permute-start | bytes 196616 | tf_op jit(solution)/shard_map/ppermute | solution.py:15
  3.7 1.5 %collective-permute-start = (bf16[4,8192]{1,0:T(4,128)(2,1)}, bf16[4,8192]{1,0:T(4,128)(2,1)S(1)}, u32[]{:S(2)}, u32[]{:S(2)}) collective-permute-start(bf16[4,8192]{1,0:T(4,128)(2,1)} %param.6), channel_id=1, source_target_pairs={{0,1},{1,0},{2,3},{3,2},{4,5},{5,4},{6,7},{7,6},{8,9},{9,8},{10,11... | collective-permute-start | bytes 196616 | tf_op jit(solution)/shard_map/ppermute | solution.py:15
  5.2 2.5 %collective-permute-start.5 = (bf16[4,8192]{1,0:T(4,128)(2,1)}, bf16[4,8192]{1,0:T(4,128)(2,1)S(1)}, u32[]{:S(2)}, u32[]{:S(2)}) collective-permute-start(bf16[4,8192]{1,0:T(4,128)(2,1)} %param.6), channel_id=1, source_target_pairs={{0,6},{1,7},{2,4},{3,5},{4,2},{5,3},{6,0},{7,1},{8,14},{9,15},{10,... | collective-permute-start | bytes 196616 | tf_op jit(solution)/shard_map/ppermute | solution.py:15
  7.7 0.1 collective-permute-start.3
  7.8 0.9 %convert_reduce_fusion.1 = s32[64]{0:T(128)S(1)} fusion(s32[64]{0:T(128)} %param.10), kind=kLoop, calls=%fused_computation.78 | loop fusion | flops 12224 | bytes 512 | tf_op jit(solution)/shard_map/reduce_sum | solution.py:57
  8.8 0.9 %bitcast_dynamic-update-slice_fusion.7 = bf16[8,4,8192]{2,1,0:T(4,128)(2,1)S(1)} fusion(bf16[4,8192]{1,0:T(4,128)(2,1)} %param.6), kind=kLoop, calls=%fused_computation.42 | loop fusion | bytes 131072
  9.7 0.7 dynamic_slice.72
  10.4 0.1 convert_reduce_fusion
  10.5 0.7 select_reduce_fusion
  11.3 0.7 fusion.31
  12.1 0.6 collective-permute-start.2
  12.7 1.5 %collective-permute-start.6 = (bf16[4,8192]{1,0:T(4,128)(2,1)S(1)}, bf16[4,8192]{1,0:T(4,128)(2,1)S(1)}, u32[]{:S(2)}, u32[]{:S(2)}) collective-permute-start(bf16[4,8192]{1,0:T(4,128)(2,1)S(1)} %collective-permute-done.5), channel_id=1, source_target_pairs={{0,1},{1,0},{2,3},{3,2},{4,5},{5,4},{6,7},{7,6},{8,9},{9,8},{10,11... | collective-permute-start | bytes 196616 | tf_op jit(solution)/shard_map/ppermute | solution.py:15
  14.2 0.6 collective-permute-start.4
  14.9 1.7 %collective-permute-done.2 = bf16[4,8192]{1,0:T(4,128)(2,1)S(1)} collective-permute-done((bf16[4,8192]{1,0:T(4,128)(2,1)S(1)}, bf16[4,8192]{1,0:T(4,128)(2,1)S(1)}, u32[]{:S(2)}, u32[]{:S(2)}) %collective-permute-start.2) | collective-permute-done | bytes 65568 | tf_op jit(solution)/shard_map/ppermute | solution.py:15
  16.7 1.9 %collective-permute-done.4 = bf16[4,8192]{1,0:T(4,128)(2,1)S(1)} collective-permute-done((bf16[4,8192]{1,0:T(4,128)(2,1)S(1)}, bf16[4,8192]{1,0:T(4,128)(2,1)S(1)}, u32[]{:S(2)}, u32[]{:S(2)}) %collective-permute-start.4) | collective-permute-done | bytes 65568 | tf_op jit(solution)/shard_map/ppermute | solution.py:15
  18.7 0.2 dynamic-slice_bitcast_fusion
  18.9 0.3 concatenate.14
  19.3 3.0 %fusion.3 = f32[32,256]{1,0:T(8,128)S(1)} fusion(bf16[32,8192]{1,0:T(8,128)(2,1)S(1)} %concatenate.14, bf16[1,8192,256]{2,1,0:T(8,128)(2,1)} %param.8), kind=kOutput, calls=%fused_computation.3 | convolution fusion | flops 134217728 | bytes 4751360 | tf_op jit(solution)/shard_map/dot_general | solution.py:104
  22.3 8.8 %convolution_bitcast_fusion = f32[4,8,8,128]{3,1,2,0:T(8,128)S(1)} fusion(bf16[32,8192]{1,0:T(8,128)(2,1)S(1)} %concatenate.14, bf16[8192,1024]{1,0:T(8,128)(2,1)} %param.7), kind=kOutput, calls=%fused_computation.7 | convolution fusion | flops 536870912 | bytes 17432576 | tf_op jit(solution)/shard_map/dot_general | solution.py:105
  31.3 0.1 fusion.65
  31.5 1.0 %collective-permute-done.7 = bf16[32,256]{1,0:T(8,128)(2,1)S(1)} collective-permute-done((bf16[32,256]{1,0:T(8,128)(2,1)S(1)}, bf16[32,256]{1,0:T(8,128)(2,1)S(1)}, u32[]{:S(2)}, u32[]{:S(2)}) %collective-permute-start.7) | collective-permute-done | bytes 16416 | tf_op jit(solution)/shard_map/ppermute | solution.py:15
  32.6 0.1 convolution_convert_fusion.1
  32.7 0.6 constant_dynamic-update-slice_fusion.15
  33.3 0.6 constant_dynamic-update-slice_fusion.14
  33.9 0.6 constant_dynamic-update-slice_fusion.13
  34.5 0.6 constant_dynamic-update-slice_fusion.12
  35.0 0.6 constant_dynamic-update-slice_fusion.11
  35.6 0.6 constant_dynamic-update-slice_fusion.10
  36.2 0.6 constant_dynamic-update-slice_fusion.9
  36.8 0.6 constant_dynamic-update-slice_fusion.8
  37.4 0.6 constant_dynamic-update-slice_fusion.7
  37.9 0.6 constant_dynamic-update-slice_fusion.6
  38.5 0.6 constant_dynamic-update-slice_fusion.5
  39.1 0.6 constant_dynamic-update-slice_fusion.4
  39.7 0.6 constant_dynamic-update-slice_fusion.3
  40.3 0.6 constant_dynamic-update-slice_fusion.2
  40.8 0.6 constant_dynamic-update-slice_fusion.1
  41.4 0.4 fusion.66
  41.8 0.6 fusion.9
  42.5 8.6 %fusion.71 = (bf16[8,4,8192]{2,0,1:T(8,128)(2,1)S(1)}, f32[8,4,8192]{2,0,1:T(8,128)S(1)}) fusion(bf16[1024,8192]{1,0:T(8,128)(2,1)} %param.9, bf16[8,4,1024]{2,1,0:T(4,128)(2,1)S(1)} %dot_general.24), kind=kOutput, calls=%fused_computation.145 | convolution fusion | flops 537133056 | bytes 18415616 | tf_op jit(solution)/shard_map/dot_general | solution.py:147
  51.1 1.0 %constant_dynamic-slice_fusion.6 = (bf16[1,4,8192]{2,0,1:T(2,128)(2,1)S(1)}, bf16[1,4,8192]{2,0,1:T(2,128)(2,1)S(1)}, bf16[1,4,8192]{2,0,1:T(2,128)(2,1)S(1)}, b...) fusion(bf16[8,4,8192]{2,0,1:T(8,128)(2,1)S(1)} %get-tuple-eleme, ...), kind=kLoop, calls=%fused_computation.104 | loop fusion | bytes 917532 | tf_op jit(solution)/shard_map/jit(dynamic_index_in_dim)/dynamic_slice | solution.py:49
  52.1 0.1 copy.51
  52.2 0.1 copy.52
  52.3 2.9 %collective-permute-start.9 = (bf16[4,8192]{1,0:T(4,128)(2,1)S(1)}, bf16[4,8192]{1,0:T(4,128)(2,1)S(1)}, u32[]{:S(2)}, u32[]{:S(2)}) collective-permute-start(bf16[4,8192]{1,0:T(4,128)(2,1)S(1)} %bitcast.189), channel_id=1, source_target_pairs={{0,6},{1,7},{2,4},{3,5},{4,2},{5,3},{6,0},{7,1},{8,14},{9,15},{10,... | collective-permute-start | bytes 196616 | tf_op jit(solution)/shard_map/ppermute | solution.py:15
  55.2 0.5 collective-permute-start.10
  55.7 0.6 constant_dynamic-update-slice_fusion
  56.3 4.7 %all-to-all-start = ((bf16[16,1,8,128]{3,2,1,0:T(8,128)(2,1)}), bf16[16,1,8,128]{3,2,1,0:T(8,128)(2,1)S(1)}, u32[]{:S(2)}, u32[]{:S(2)}) async-start(bf16[16,1,8,128]{3,2,1,0:T(8,128)(2,1)} %constant_dynamic-update-slice_fusion), calls=%async_computation | async-start | bytes 65536 | tf_op jit(solution)/shard_map/all_to_all | solution.py:139
  61.0 0.1 copy.53
  61.1 0.1 copy.47
  61.2 0.1 copy.48
  61.3 0.1 copy.49
  61.4 0.1 copy.50
  61.5 2.9 %collective-permute-start.11 = (bf16[4,8192]{1,0:T(4,128)(2,1)S(1)}, bf16[4,8192]{1,0:T(4,128)(2,1)S(1)}, u32[]{:S(2)}, u32[]{:S(2)}) collective-permute-start(bf16[4,8192]{1,0:T(4,128)(2,1)S(1)} %bitcast.190), channel_id=1, source_target_pairs={{0,4},{1,5},{2,6},{3,7},{4,0},{5,1},{6,2},{7,3},{8,12},{9,13},{10,... | collective-permute-start | bytes 196616 | tf_op jit(solution)/shard_map/ppermute | solution.py:15
  64.4 2.4 %collective-permute-start.12 = (bf16[4,8192]{1,0:T(4,128)(2,1)S(1)}, bf16[4,8192]{1,0:T(4,128)(2,1)S(1)}, u32[]{:S(2)}, u32[]{:S(2)}) collective-permute-start(bf16[4,8192]{1,0:T(4,128)(2,1)S(1)} %bitcast.188), channel_id=1, source_target_pairs={{0,3},{1,2},{2,1},{3,0},{4,7},{5,6},{6,5},{7,4},{8,11},{9,10},{10,... | collective-permute-start | bytes 196616 | tf_op jit(solution)/shard_map/ppermute | solution.py:15
  66.8 0.6 collective-permute-start.13
  67.3 0.6 collective-permute-start.14
  67.9 2.4 %collective-permute-start.8 = (bf16[4,8192]{1,0:T(4,128)(2,1)S(1)}, bf16[4,8192]{1,0:T(4,128)(2,1)S(1)}, u32[]{:S(2)}, u32[]{:S(2)}) collective-permute-start(bf16[4,8192]{1,0:T(4,128)(2,1)S(1)} %bitcast.184), channel_id=1, source_target_pairs={{0,7},{1,6},{2,5},{3,4},{4,3},{5,2},{6,1},{7,0},{8,15},{9,14},{10,... | collective-permute-start | bytes 196616 | tf_op jit(solution)/shard_map/ppermute | solution.py:15
  70.3 0.1 constant_dynamic-slice_fusion.7
  70.4 0.4 collective-permute-done.12
  70.8 0.4 collective-permute-done.13
  71.2 0.4 collective-permute-done.14
  71.6 3.3 %collective-permute-done.8 = bf16[4,8192]{1,0:T(4,128)(2,1)S(1)} collective-permute-done((bf16[4,8192]{1,0:T(4,128)(2,1)S(1)}, bf16[4,8192]{1,0:T(4,128)(2,1)S(1)}, u32[]{:S(2)}, u32[]{:S(2)}) %collective-permute-start.8) | collective-permute-done | bytes 65568 | tf_op jit(solution)/shard_map/ppermute | solution.py:15
  74.9 0.8 %fusion.16 = bf16[4,8192]{1,0:T(4,128)(2,1)} fusion(bf16[4,8192]{1,0:T(4,128)(2,1)S(1)} %collective-permute-done.14, bf16[4,8192]{1,0:T(4,128)(2,1)S(1)} %collective-permute-done.13, bf16[4,8192]{1,0:T(4,128)(2,1)S(1)} %collective-permute-done.12, bf16[4,8192]{1,0:T(4,128)(2,1)S(1)} %collective-permute-done.11, ...), kind=kLoop, calls=%fused_computation.24 | loop fusion | flops 491520 | bytes 655360 | tf_op jit(solution)/shard_map/convert_element_type | solution.py:148
  75.7 0.6 copy.77
  (33 shorter events, 0.9 us)
Async XLA Ops:
  0.6 11.5 %collective-permute-start.1 = (bf16[4,8192]{1,0:T(4,128)(2,1)}, bf16[4,8192]{1,0:T(4,128)(2,1)S(1)}, u32[]{:S(2)}, u32[]{:S(2)}) collective-permute-start(bf16[4,8192]{1,0:T(4,128)(2,1)} %param.6), channel_id=1, source_target_pairs={{0,2},{1,3},{2,0},{3,1},{4,6},{5,7},{6,4},{7,5},{8,10},{9,11},{10,... | collective-permute-start | bytes 196616 | tf_op jit(solution)/shard_map/ppermute | solution.py:15
  3.7 11.1 %collective-permute-start = (bf16[4,8192]{1,0:T(4,128)(2,1)}, bf16[4,8192]{1,0:T(4,128)(2,1)S(1)}, u32[]{:S(2)}, u32[]{:S(2)}) collective-permute-start(bf16[4,8192]{1,0:T(4,128)(2,1)} %param.6), channel_id=1, source_target_pairs={{0,1},{1,0},{2,3},{3,2},{4,5},{5,4},{6,7},{7,6},{8,9},{9,8},{10,11... | collective-permute-start | bytes 196616 | tf_op jit(solution)/shard_map/ppermute | solution.py:15
  5.2 7.5 %collective-permute-start.5 = (bf16[4,8192]{1,0:T(4,128)(2,1)}, bf16[4,8192]{1,0:T(4,128)(2,1)S(1)}, u32[]{:S(2)}, u32[]{:S(2)}) collective-permute-start(bf16[4,8192]{1,0:T(4,128)(2,1)} %param.6), channel_id=1, source_target_pairs={{0,6},{1,7},{2,4},{3,5},{4,2},{5,3},{6,0},{7,1},{8,14},{9,15},{10,... | collective-permute-start | bytes 196616 | tf_op jit(solution)/shard_map/ppermute | solution.py:15
  7.7 6.5 %collective-permute-start.3 = (bf16[4,8192]{1,0:T(4,128)(2,1)}, bf16[4,8192]{1,0:T(4,128)(2,1)S(1)}, u32[]{:S(2)}, u32[]{:S(2)}) collective-permute-start(bf16[4,8192]{1,0:T(4,128)(2,1)} %param.6), channel_id=1, source_target_pairs={{0,4},{1,5},{2,6},{3,7},{4,0},{5,1},{6,2},{7,3},{8,12},{9,13},{10,... | collective-permute-start | bytes 196616 | tf_op jit(solution)/shard_map/ppermute | solution.py:15
  12.1 4.5 %collective-permute-start.2 = (bf16[4,8192]{1,0:T(4,128)(2,1)S(1)}, bf16[4,8192]{1,0:T(4,128)(2,1)S(1)}, u32[]{:S(2)}, u32[]{:S(2)}) collective-permute-start(bf16[4,8192]{1,0:T(4,128)(2,1)S(1)} %collective-permute-done.1), channel_id=1, source_target_pairs={{0,1},{1,0},{2,3},{3,2},{4,5},{5,4},{6,7},{7,6},{8,9},{9,8},{10,11... | collective-permute-start | bytes 196616 | tf_op jit(solution)/shard_map/ppermute | solution.py:15
  12.7 5.9 %collective-permute-start.6 = (bf16[4,8192]{1,0:T(4,128)(2,1)S(1)}, bf16[4,8192]{1,0:T(4,128)(2,1)S(1)}, u32[]{:S(2)}, u32[]{:S(2)}) collective-permute-start(bf16[4,8192]{1,0:T(4,128)(2,1)S(1)} %collective-permute-done.5), channel_id=1, source_target_pairs={{0,1},{1,0},{2,3},{3,2},{4,5},{5,4},{6,7},{7,6},{8,9},{9,8},{10,11... | collective-permute-start | bytes 196616 | tf_op jit(solution)/shard_map/ppermute | solution.py:15
  14.2 4.3 %collective-permute-start.4 = (bf16[4,8192]{1,0:T(4,128)(2,1)S(1)}, bf16[4,8192]{1,0:T(4,128)(2,1)S(1)}, u32[]{:S(2)}, u32[]{:S(2)}) collective-permute-start(bf16[4,8192]{1,0:T(4,128)(2,1)S(1)} %collective-permute-done.3), channel_id=1, source_target_pairs={{0,1},{1,0},{2,3},{3,2},{4,5},{5,4},{6,7},{7,6},{8,9},{9,8},{10,11... | collective-permute-start | bytes 196616 | tf_op jit(solution)/shard_map/ppermute | solution.py:15
  31.3 1.2 %collective-permute-start.7 = (bf16[32,256]{1,0:T(8,128)(2,1)S(1)}, bf16[32,256]{1,0:T(8,128)(2,1)S(1)}, u32[]{:S(2)}, u32[]{:S(2)}) collective-permute-start(bf16[32,256]{1,0:T(8,128)(2,1)S(1)} %pad_maximum_fusion), channel_id=1, source_target_pairs={{0,8},{8,0},{1,9},{9,1},{2,10},{10,2},{3,11},{11,3},{4,12},{12,4},... | collective-permute-start | bytes 49160 | tf_op jit(solution)/shard_map/ppermute | solution.py:15
  52.3 15.0 %collective-permute-start.9 = (bf16[4,8192]{1,0:T(4,128)(2,1)S(1)}, bf16[4,8192]{1,0:T(4,128)(2,1)S(1)}, u32[]{:S(2)}, u32[]{:S(2)}) collective-permute-start(bf16[4,8192]{1,0:T(4,128)(2,1)S(1)} %bitcast.189), channel_id=1, source_target_pairs={{0,6},{1,7},{2,4},{3,5},{4,2},{5,3},{6,0},{7,1},{8,14},{9,15},{10,... | collective-permute-start | bytes 196616 | tf_op jit(solution)/shard_map/ppermute | solution.py:15
  55.2 12.7 %collective-permute-start.10 = (bf16[4,8192]{1,0:T(4,128)(2,1)S(1)}, bf16[4,8192]{1,0:T(4,128)(2,1)S(1)}, u32[]{:S(2)}, u32[]{:S(2)}) collective-permute-start(bf16[4,8192]{1,0:T(4,128)(2,1)S(1)} %bitcast.187), channel_id=1, source_target_pairs={{0,5},{1,4},{2,7},{3,6},{4,1},{5,0},{6,3},{7,2},{8,13},{9,12},{10,... | collective-permute-start | bytes 196616 | tf_op jit(solution)/shard_map/ppermute | solution.py:15
  56.3 14.1 %all-to-all-start = ((bf16[16,1,8,128]{3,2,1,0:T(8,128)(2,1)}), bf16[16,1,8,128]{3,2,1,0:T(8,128)(2,1)S(1)}, u32[]{:S(2)}, u32[]{:S(2)}) async-start(bf16[16,1,8,128]{3,2,1,0:T(8,128)(2,1)} %constant_dynamic-update-slice_fusion), calls=%async_computation | async-start | bytes 65536 | tf_op jit(solution)/shard_map/all_to_all | solution.py:139
  61.5 8.9 %collective-permute-start.11 = (bf16[4,8192]{1,0:T(4,128)(2,1)S(1)}, bf16[4,8192]{1,0:T(4,128)(2,1)S(1)}, u32[]{:S(2)}, u32[]{:S(2)}) collective-permute-start(bf16[4,8192]{1,0:T(4,128)(2,1)S(1)} %bitcast.190), channel_id=1, source_target_pairs={{0,4},{1,5},{2,6},{3,7},{4,0},{5,1},{6,2},{7,3},{8,12},{9,13},{10,... | collective-permute-start | bytes 196616 | tf_op jit(solution)/shard_map/ppermute | solution.py:15
  64.4 6.4 %collective-permute-start.12 = (bf16[4,8192]{1,0:T(4,128)(2,1)S(1)}, bf16[4,8192]{1,0:T(4,128)(2,1)S(1)}, u32[]{:S(2)}, u32[]{:S(2)}) collective-permute-start(bf16[4,8192]{1,0:T(4,128)(2,1)S(1)} %bitcast.188), channel_id=1, source_target_pairs={{0,3},{1,2},{2,1},{3,0},{4,7},{5,6},{6,5},{7,4},{8,11},{9,10},{10,... | collective-permute-start | bytes 196616 | tf_op jit(solution)/shard_map/ppermute | solution.py:15
  66.8 4.4 %collective-permute-start.13 = (bf16[4,8192]{1,0:T(4,128)(2,1)S(1)}, bf16[4,8192]{1,0:T(4,128)(2,1)S(1)}, u32[]{:S(2)}, u32[]{:S(2)}) collective-permute-start(bf16[4,8192]{1,0:T(4,128)(2,1)S(1)} %bitcast.186), channel_id=1, source_target_pairs={{0,2},{1,3},{2,0},{3,1},{4,6},{5,7},{6,4},{7,5},{8,10},{9,11},{10,... | collective-permute-start | bytes 196616 | tf_op jit(solution)/shard_map/ppermute | solution.py:15
  67.3 4.3 %collective-permute-start.14 = (bf16[4,8192]{1,0:T(4,128)(2,1)S(1)}, bf16[4,8192]{1,0:T(4,128)(2,1)S(1)}, u32[]{:S(2)}, u32[]{:S(2)}) collective-permute-start(bf16[4,8192]{1,0:T(4,128)(2,1)S(1)} %bitcast.185), channel_id=1, source_target_pairs={{0,1},{1,0},{2,3},{3,2},{4,5},{5,4},{6,7},{7,6},{8,9},{9,8},{10,11... | collective-permute-start | bytes 196616 | tf_op jit(solution)/shard_map/ppermute | solution.py:15
  67.9 7.0 %collective-permute-start.8 = (bf16[4,8192]{1,0:T(4,128)(2,1)S(1)}, bf16[4,8192]{1,0:T(4,128)(2,1)S(1)}, u32[]{:S(2)}, u32[]{:S(2)}) collective-permute-start(bf16[4,8192]{1,0:T(4,128)(2,1)S(1)} %bitcast.184), channel_id=1, source_target_pairs={{0,7},{1,6},{2,5},{3,4},{4,3},{5,2},{6,1},{7,0},{8,15},{9,14},{10,... | collective-permute-start | bytes 196616 | tf_op jit(solution)/shard_map/ppermute | solution.py:15
